TPU v7x, 32 devices: a whole 2x2x4 slice. The times are simulated.
32 devices in a mesh: mode: 4 (over y, x), mesh: 8 (over z, core).
Axes of the slice: x: 2, y: 2, z: 4, core: 2. Of those that a mesh axis runs over, the one named last changes fastest.
Arguments:
- velocity: float32 [3, 2, 64, 20480], P(None, None, 'mode', 'mesh'), may hold values from -2.1 to 2.1
- magnetic: float32 [3, 2, 64, 20480], P(None, None, 'mode', 'mesh'), may hold values from -2.1 to 2.1
- leaf_inverse: bfloat16 [64, 160, 128, 128], P('mode', 'mesh'), may hold values from -1 to 2
- leaf_coupling: bfloat16 [64, 128, 20480], P('mode', None, 'mesh'), may hold values from -0.05908203 to 0.05908203
- separator_inverse: bfloat16 [64, 1024, 128], P('mode', 'mesh'), may hold values from -1 to 2
- separator_coupling: bfloat16 [64, 1024, 128], P('mode', 'mesh'), may hold values from -0.26367188 to 0.26367188
- separator_source: float32 [2, 64, 1024], P(None, 'mode', 'mesh'), may hold values from -6 to 6
- front_rows: int32 [8, 2, 128], P('mesh'), may hold values from 0 to 127, each once within a row
Outputs:
- nonlinear: float32 [3, 2, 64, 20480], P(None, None, 'mode', 'mesh')
- azimuthal_field: float32 [2, 64, 20480], P(None, 'mode', 'mesh')
- separator_solution: float32 [2, 64, 1024], P(None, 'mode', 'mesh')
Inputs may be any that keep to these rules, and one draw needn't show every extreme that they name: front_rows[p, 0] and front_rows[p, 1] each hold every number below 128 once.
All inputs are finite; a program needn't handle non-finite values.
Results may differ from a plain program's by a relative error of at most 0.015.
Values may be sent and summed in bfloat16 or wider, within the bound.
No kernel may reach another device: no remote copies, remote signals or barrier semaphores. Data moves between devices by JAX's collectives and lax.ppermute only.
A program may use at most 128 MiB of HBM per device.

v0:
```python
import jax
import jax.numpy as jnp
from jax import lax
from jax.sharding import PartitionSpec as P

M = 64
NPHI = 192
highest = lax.Precision.HIGHEST
dt_step = 0.5


def tables():
    angles = jnp.arange(NPHI, dtype=jnp.int32)[:, None]
    orders = jnp.arange(M, dtype=jnp.int32)[None, :]
    phase = (angles * orders % NPHI).astype(jnp.float32) * (2.0 * jnp.pi / NPHI)
    forward = jnp.stack([jnp.cos(phase), jnp.sin(phase)], axis=1)
    weights = jnp.where(orders == 0, 1.0, 2.0).astype(jnp.float32) / NPHI
    backward = jnp.stack([(jnp.cos(phase) * weights).T, (jnp.sin(phase) * weights).T], axis=0)
    return (forward, backward)


def cross_terms(first, second):
    return jnp.stack(
        [
            first[1] * second[2] - first[2] * second[1],
            first[2] * second[0] - first[0] * second[2],
            first[0] * second[1] - first[1] * second[0],
        ]
    )


def forward_fields(forward, velocity, magnetic):
    return (
        jnp.einsum("kam,camn->ckn", forward, velocity, precision=highest),
        jnp.einsum("kam,camn->ckn", forward, magnetic, precision=highest),
    )


def gather_children(values):
    return lax.all_gather(values, "mesh", axis=2, tiled=True)


def gather_parents(values):
    return lax.all_gather(values, "mesh", axis=2, tiled=True)


def block_of(whole, index, partitions, sep_rows):
    start = (jnp.clip(index, 0, partitions - 1) * sep_rows).astype(jnp.int32)
    return lax.dynamic_slice_in_dim(whole, start, sep_rows, 2)


def shards(
    velocity,
    magnetic,
    leaf_inverse,
    leaf_coupling,
    separator_inverse,
    separator_coupling,
    separator_source,
    front_rows,
):
    modes_dev = velocity.shape[2]
    nodes_dev = velocity.shape[3]
    forward, backward = tables()
    spread_velocity, spread_magnetic = (
        lax.all_to_all(
            velocity.astype(jnp.bfloat16), "mode", split_axis=3, concat_axis=2, tiled=True
        ).astype(velocity.dtype),
        lax.all_to_all(
            magnetic.astype(jnp.bfloat16), "mode", split_axis=3, concat_axis=2, tiled=True
        ).astype(magnetic.dtype),
    )
    phys_velocity, phys_magnetic = forward_fields(forward, spread_velocity, spread_magnetic)
    local_terms = jnp.einsum(
        "amk,ckn->camn", backward, cross_terms(phys_velocity, phys_magnetic), precision=highest
    )
    nonlinear = lax.all_to_all(
        local_terms.astype(jnp.bfloat16), "mode", split_axis=2, concat_axis=3, tiled=True
    ).astype(local_terms.dtype)
    blocks_dev = leaf_inverse.shape[1]
    block_width = leaf_inverse.shape[2]
    sep_rows = separator_source.shape[2]
    source = (magnetic[1] + dt_step * nonlinear[1]).astype(jnp.bfloat16)
    leaf_solved = (
        jnp.einsum(
            "mkij,cmkj->cmki",
            leaf_inverse,
            source.reshape(2, modes_dev, blocks_dev, block_width),
            preferred_element_type=jnp.float32,
        )
        .reshape(2, modes_dev, nodes_dev)
        .astype(jnp.bfloat16)
    )
    row_order = front_rows[0]
    leaf_map = jnp.take(leaf_coupling, row_order[0], axis=1)
    upward_map = jnp.take(separator_coupling, row_order[1], axis=1)
    leaf_update = jnp.einsum(
        "mij,cmj->cmi", leaf_map, leaf_solved, preferred_element_type=jnp.float32
    )
    partitions = lax.axis_size("mesh")
    levels = partitions.bit_length() - 1
    position = lax.axis_index("mesh")
    depth_now = sum(
        [(position % 2**bit_now == 0).astype(jnp.int32) for bit_now in range(1, levels + 1)]
    )
    level_here = depth_now + 1

    def settle(arrived, height, reduced, outgoing):
        fresh = jnp.einsum(
            "mij,cmj->cmi",
            separator_inverse,
            (separator_source - arrived).astype(jnp.bfloat16),
            preferred_element_type=jnp.float32,
        ).astype(jnp.bfloat16)
        sending = jnp.einsum("mij,cmj->cmi", upward_map, fresh, preferred_element_type=jnp.float32)
        active = level_here == height
        return (jnp.where(active, fresh, reduced), jnp.where(active, sending, outgoing))

    reduced = jnp.zeros(separator_source.shape, jnp.bfloat16)
    outgoing = jnp.zeros(separator_source.shape, jnp.float32)
    everyone = gather_children(leaf_update)
    arrived = block_of(everyone, position - 1, partitions, sep_rows) + block_of(
        everyone, position, partitions, sep_rows
    )
    reduced, outgoing = settle(arrived, 1, reduced, outgoing)
    for height in range(2, levels + 1):
        gap = 2 ** (height - 2)
        everyone = gather_children(outgoing)
        arrived = block_of(everyone, position - gap, partitions, sep_rows) + block_of(
            everyone, position + gap, partitions, sep_rows
        )
        reduced, outgoing = settle(arrived, height, reduced, outgoing)
    everyone = gather_children(outgoing)
    reduced, outgoing = settle(
        block_of(everyone, partitions // 2, partitions, sep_rows), levels + 1, reduced, outgoing
    )
    top_value = jnp.einsum(
        "mij,cmi->cmj", separator_inverse, reduced, preferred_element_type=jnp.float32
    )
    solution = jnp.where(
        level_here == levels + 1, top_value, jnp.zeros(separator_source.shape, jnp.float32)
    )
    for height in range(levels, 0, -1):
        everyone = gather_parents(solution.astype(jnp.bfloat16))
        if height == levels:
            parent = position * 0
        else:
            parent = position // 2 ** (height + 1) * 2 ** (height + 1) + 2**height
        above = block_of(everyone, parent, partitions, sep_rows)
        residue = reduced.astype(jnp.float32) - jnp.einsum(
            "mij,cmi->cmj", upward_map, above, preferred_element_type=jnp.float32
        )
        fresh = jnp.einsum(
            "mij,cmi->cmj",
            separator_inverse,
            residue.astype(jnp.bfloat16),
            preferred_element_type=jnp.float32,
        )
        solution = jnp.where(level_here == height, fresh, solution)
    everyone = gather_parents(solution.astype(jnp.bfloat16))
    above = block_of(everyone, 2 * (position // 2) + 1, partitions, sep_rows)
    residue = leaf_solved.astype(jnp.float32) - jnp.einsum(
        "mij,cmi->cmj", leaf_map, above, preferred_element_type=jnp.float32
    )
    azimuthal_field = jnp.einsum(
        "mkji,cmkj->cmki",
        leaf_inverse,
        residue.astype(jnp.bfloat16).reshape(2, modes_dev, blocks_dev, block_width),
        preferred_element_type=jnp.float32,
    ).reshape(2, modes_dev, nodes_dev)
    return (nonlinear, azimuthal_field, solution)


def solution(mesh):
    in_specs = (
        P(None, None, "mode", "mesh"),
        P(None, None, "mode", "mesh"),
        P("mode", "mesh", None, None),
        P("mode", None, "mesh"),
        P("mode", "mesh", None),
        P("mode", "mesh", None),
        P(None, "mode", "mesh"),
        P("mesh", None, None),
    )
    out_specs = (P(None, None, "mode", "mesh"), P(None, "mode", "mesh"), P(None, "mode", "mesh"))
    return jax.shard_map(shards, mesh=mesh, in_specs=in_specs, out_specs=out_specs, check_vma=False)
```

profile of v0, /device:TPU:0, one launch (start us, length us, event | category | flops | bytes accessed | tf_op | source)
XLA Modules:
  0.0 205.2 jit_solution(15129035748217924793)
XLA Ops:
  2.0 5.2 %copy.84 = bf16[3,2,16,2560]{2,0,1,3:T(4,128)(2,1)} copy(bf16[3,2,16,2560]{3,2,1,0:T(8,128)(2,1)S(1)} %convert_element_type.163) | data formatting | bytes 983040 | tf_op jit(solution)/shard_map/convert_element_type | solution.py:70
  7.2 6.7 %reshape.281 = bf16[4,2,30720]{2,1,0:T(2,128)(2,1)} reshape(bf16[2560,2,3,16]{3,2,1,0:T(4,128)(2,1)} %bitcast.190) | data formatting | bytes 983040
  13.9 5.2 %all-to-all-start.1 = ((bf16[4,2,30720]{2,1,0:T(2,128)(2,1)}), bf16[4,2,30720]{2,1,0:T(2,128)(2,1)S(1)}, u32[]{:S(2)}, u32[]{:S(2)}) async-start(bf16[4,2,30720]{2,1,0:T(2,128)(2,1)} %reshape.281), calls=%async_computation.1 | async-start | bytes 983040 | tf_op jit(solution)/shard_map/all_to_all | solution.py:69
  19.1 5.2 %copy.82 = bf16[3,2,16,2560]{2,0,1,3:T(4,128)(2,1)} copy(bf16[3,2,16,2560]{3,2,1,0:T(8,128)(2,1)S(1)} %convert_element_type.162) | data formatting | bytes 983040 | tf_op jit(solution)/shard_map/convert_element_type | solution.py:67
  24.3 6.7 %reshape.279 = bf16[4,2,30720]{2,1,0:T(2,128)(2,1)} reshape(bf16[2560,2,3,16]{3,2,1,0:T(4,128)(2,1)} %bitcast.191) | data formatting | bytes 983040
  31.0 4.2 %all-to-all-start = ((bf16[4,2,30720]{2,1,0:T(2,128)(2,1)}), bf16[4,2,30720]{2,1,0:T(2,128)(2,1)S(1)}, u32[]{:S(2)}, u32[]{:S(2)}) async-start(bf16[4,2,30720]{2,1,0:T(2,128)(2,1)} %reshape.279), calls=%async_computation | async-start | bytes 983040 | tf_op jit(solution)/shard_map/all_to_all | solution.py:66
  35.8 6.0 %reshape.282 = bf16[2560,2,3,16]{3,2,1,0:T(4,128)(2,1)} reshape(bf16[4,2,30720]{2,1,0:T(2,128)(2,1)S(1)} %all-to-all-done.1) | data formatting | bytes 983040
  41.8 5.8 %copy.85 = bf16[3,2,16,4,640]{4,2,3,1,0:T(8,128)(2,1)S(1)} copy(bf16[3,2,16,4,640]{2,0,1,4,3:T(4,128)(2,1)} %bitcast.192) | data formatting | bytes 983040 | tf_op jit(solution)/shard_map/all_to_all | solution.py:69
  47.5 6.0 %reshape.280 = bf16[2560,2,3,16]{3,2,1,0:T(4,128)(2,1)} reshape(bf16[4,2,30720]{2,1,0:T(2,128)(2,1)S(1)} %all-to-all-done) | data formatting | bytes 983040
  53.5 5.8 %copy.83 = bf16[3,2,16,4,640]{4,2,3,1,0:T(8,128)(2,1)S(1)} copy(bf16[3,2,16,4,640]{2,0,1,4,3:T(4,128)(2,1)} %bitcast.193) | data formatting | bytes 983040 | tf_op jit(solution)/shard_map/all_to_all | solution.py:66
  63.5 4.2 %all-to-all-start.2 = ((bf16[3,2,64,640]{3,1,0,2:T(2,128)(2,1)}), bf16[3,2,64,640]{3,1,0,2:T(2,128)(2,1)S(1)}, u32[]{:S(2)}, u32[]{:S(2)}) async-start(bf16[3,2,64,640]{3,1,0,2:T(2,128)(2,1)} %copy.86), calls=%async_computation.2 | async-start | bytes 983040 | tf_op jit(solution)/shard_map/all_to_all | solution.py:77
  67.9 2.8 %gather_fusion.1 = bf16[128,16,128]{2,0,1:T(8,128)(2,1)S(1)} fusion(bf16[16,128,128]{2,1,0:T(8,128)(2,1)S(1)} %copy-done, s32[1024]{0:T(1024)S(1)} %pad_clamp_fusion), kind=kCustom, calls=%fused_computation.1 | custom fusion | bytes 1049088 | tf_op jit(solution)/shard_map/jit(_take)/gather | solution.py:96
  70.6 24.7 %gather_fusion = bf16[128,16,2560]{2,0,1:T(8,128)(2,1)} fusion(bf16[16,128,2560]{2,1,0:T(8,128)(2,1)} %param.11, s32[1024]{0:T(1024)S(1)} %pad_clamp_fusion.1), kind=kCustom, calls=%fused_computation | custom fusion | bytes 20972032 | tf_op jit(solution)/shard_map/jit(_take)/gather | solution.py:95
  97.6 9.0 %fusion.20 = bf16[2,16,2560]{2,0,1:T(2,128)(2,1)S(1)} fusion(bf16[16,20,128,128]{3,2,1,0:T(8,128)(2,1)} %param.10, bf16[2,16,20,128]{3,2,1,0:T(8,128)(2,1)S(1)} %convert_element_type.172), kind=kOutput, calls=%fused_computation.22 | convolution fusion | flops 21053440 | bytes 10813440 | tf_op jit(solution)/shard_map/mkij,cmkj->cmki/dot_general | solution.py:85
  106.7 2.9 %fusion.26 = f32[2,16,128]{2,0,1:T(2,128)S(1)} fusion(bf16[2,16,2560]{2,0,1:T(2,128)(2,1)S(1)} %fusion.20, bf16[128,16,2560]{2,0,1:T(8,128)(2,1)S(1)} %copy-done.2, pred[128]{0:T(512)(128)(4,1)S(1)} %get-tuple-element.25), kind=kOutput, calls=%fused_computation.24 | convolution fusion | flops 26214400 | bytes 10666112 | tf_op jit(solution)/shard_map/mij,cmj->cmi/dot_general | solution.py:97
  109.5 12.5 %all_gather.24 = f32[2,16,1024]{2,0,1:T(2,128)S(1)} all-gather(f32[2,16,128]{2,0,1:T(2,128)S(1)} %fusion.26), channel_id=1, replica_groups=mesh['mode'=4,'mesh'=8] {'mesh'}, dimensions={2}, use_global_device_ids=true | all-gather | bytes 147456 | tf_op jit(solution)/shard_map/all_gather | solution.py:40
  122.9 9.3 %all_gather.25 = f32[2,16,1024]{2,0,1:T(2,128)S(1)} all-gather(f32[2,16,128]{2,0,1:T(2,128)S(1)} %fusion.35), channel_id=1, replica_groups=mesh['mode'=4,'mesh'=8] {'mesh'}, dimensions={2}, use_global_device_ids=true | all-gather | bytes 147456 | tf_op jit(solution)/shard_map/all_gather | solution.py:40
  133.0 10.6 %all_gather.26 = f32[2,16,1024]{2,0,1:T(2,128)S(1)} all-gather(f32[2,16,128]{2,0,1:T(2,128)S(1)} %fusion.34), channel_id=1, replica_groups=mesh['mode'=4,'mesh'=8] {'mesh'}, dimensions={2}, use_global_device_ids=true | all-gather | bytes 147456 | tf_op jit(solution)/shard_map/all_gather | solution.py:40
  144.4 9.3 %all_gather.27 = f32[2,16,1024]{2,0,1:T(2,128)S(1)} all-gather(f32[2,16,128]{2,0,1:T(2,128)S(1)} %fusion.33), channel_id=1, replica_groups=mesh['mode'=4,'mesh'=8] {'mesh'}, dimensions={2}, use_global_device_ids=true | all-gather | bytes 147456 | tf_op jit(solution)/shard_map/all_gather | solution.py:40
  154.3 10.3 %all_gather.28 = bf16[2,16,1024]{2,0,1:T(2,128)(2,1)S(1)} all-gather(bf16[2,16,128]{2,0,1:T(2,128)(2,1)S(1)} %convert_bitcast_fusion.2), channel_id=1, replica_groups=mesh['mode'=4,'mesh'=8] {'mesh'}, dimensions={2}, use_global_device_ids=true | all-gather | bytes 73728 | tf_op jit(solution)/shard_map/all_gather | solution.py:44
  165.1 9.0 %all_gather.29 = bf16[2,16,1024]{2,0,1:T(2,128)(2,1)S(1)} all-gather(bf16[2,16,128]{2,0,1:T(2,128)(2,1)S(1)} %convert_bitcast_fusion.1), channel_id=1, replica_groups=mesh['mode'=4,'mesh'=8] {'mesh'}, dimensions={2}, use_global_device_ids=true | all-gather | bytes 73728 | tf_op jit(solution)/shard_map/all_gather | solution.py:44
  174.6 10.3 %all_gather.30 = bf16[2,16,1024]{2,0,1:T(2,128)(2,1)S(1)} all-gather(bf16[2,16,128]{2,0,1:T(2,128)(2,1)S(1)} %convert_bitcast_fusion), channel_id=1, replica_groups=mesh['mode'=4,'mesh'=8] {'mesh'}, dimensions={2}, use_global_device_ids=true | all-gather | bytes 73728 | tf_op jit(solution)/shard_map/all_gather | solution.py:44
  186.0 9.1 %all_gather.31 = bf16[2,16,1024]{2,0,1:T(2,128)(2,1)S(1)} all-gather(bf16[2,16,128]{2,0,1:T(2,128)(2,1)S(1)} %get-tuple-element.30), channel_id=1, replica_groups=mesh['mode'=4,'mesh'=8] {'mesh'}, dimensions={2}, use_global_device_ids=true | all-gather | bytes 73728 | tf_op jit(solution)/shard_map/all_gather | solution.py:44
  195.1 9.3 %convolution_bitcast_fusion.2 = f32[2,16,20,128]{3,0,2,1:T(2,128)S(1)} fusion(bf16[16,20,128,128]{3,2,1,0:T(8,128)(2,1)} %param.10, bf16[128,16,2560]{2,0,1:T(8,128)(2,1)} %gather_fusion, pred[128]{0:T(512)(128)(4,1)S(1)} %get-tuple-element.25, bf16[2,16,2560]{2,0,1:T(2,128)(2,1)S(1)} %fusion.20, bf16[2,16,1024]{2,0,1:T(2,128)(2,1)S(1)} %all_gather.31, ...), kind=kOutput, calls=%fused_computation.20 | convolution fusion | flops 47431680 | bytes 21471748 | tf_op jit(solution)/shard_map/mkji,cmkj->cmki/dot_general | solution.py:165
  (54 shorter events, 14.4 us)
Async XLA Ops:
  0.6 67.2 %copy-start = (bf16[16,128,128]{2,1,0:T(8,128)(2,1)S(1)}, bf16[16,128,128]{2,1,0:T(8,128)(2,1)}, u32[]{:S(2)}) copy-start(bf16[16,128,128]{2,1,0:T(8,128)(2,1)} %param.13) | copy-start | bytes 1572868
  0.6 18.4 %copy-start.4 = (f32[3,2,16,2560]{3,2,1,0:T(8,128)S(1)}, f32[3,2,16,2560]{3,2,1,0:T(8,128)}, u32[]{:S(2)}) copy-start(f32[3,2,16,2560]{3,2,1,0:T(8,128)} %param.8) | copy-start | bytes 2949124
  7.2 23.8 %copy-start.6 = (s32[1,2,128]{2,1,0:T(2,128)S(1)}, s32[1,2,128]{2,1,0:T(2,128)}, u32[]{:S(2)}) copy-start(s32[1,2,128]{2,1,0:T(2,128)} %param.15) | copy-start | bytes 3076
  13.9 17.1 %all-to-all-start.1 = ((bf16[4,2,30720]{2,1,0:T(2,128)(2,1)}), bf16[4,2,30720]{2,1,0:T(2,128)(2,1)S(1)}, u32[]{:S(2)}, u32[]{:S(2)}) async-start(bf16[4,2,30720]{2,1,0:T(2,128)(2,1)} %reshape.281), calls=%async_computation.1 | async-start | bytes 983040 | tf_op jit(solution)/shard_map/all_to_all | solution.py:69
  31.0 16.5 %all-to-all-start = ((bf16[4,2,30720]{2,1,0:T(2,128)(2,1)}), bf16[4,2,30720]{2,1,0:T(2,128)(2,1)S(1)}, u32[]{:S(2)}, u32[]{:S(2)}) async-start(bf16[4,2,30720]{2,1,0:T(2,128)(2,1)} %reshape.279), calls=%async_computation | async-start | bytes 983040 | tf_op jit(solution)/shard_map/all_to_all | solution.py:66
  63.5 31.8 %all-to-all-start.2 = ((bf16[3,2,64,640]{3,1,0,2:T(2,128)(2,1)}), bf16[3,2,64,640]{3,1,0,2:T(2,128)(2,1)S(1)}, u32[]{:S(2)}, u32[]{:S(2)}) async-start(bf16[3,2,64,640]{3,1,0,2:T(2,128)(2,1)} %copy.86), calls=%async_computation.2 | async-start | bytes 983040 | tf_op jit(solution)/shard_map/all_to_all | solution.py:77
  96.6 10.1 %copy-start.2 = (bf16[128,16,2560]{2,0,1:T(8,128)(2,1)S(1)}, bf16[128,16,2560]{2,0,1:T(8,128)(2,1)}, u32[]{:S(2)}) copy-start(bf16[128,16,2560]{2,0,1:T(8,128)(2,1)} %gather_fusion) | copy-start | bytes 31457284
  106.6 15.4 %copy-start.3 = (bf16[16,128,128]{2,1,0:T(8,128)(2,1)S(1)}, bf16[16,128,128]{2,1,0:T(8,128)(2,1)}, u32[]{:S(2)}) copy-start(bf16[16,128,128]{2,1,0:T(8,128)(2,1)} %param.12) | copy-start | bytes 1572868
  106.6 15.4 %copy-start.5 = (f32[2,16,128]{2,1,0:T(8,128)S(1)}, f32[2,16,128]{2,1,0:T(8,128)}, u32[]{:S(2)}) copy-start(f32[2,16,128]{2,1,0:T(8,128)} %param.14) | copy-start | bytes 49156
  186.0 19.3 %copy-start.1 = (bf16[16,128,128]{2,1,0:T(8,128)(2,1)S(1)}, bf16[16,128,128]{2,1,0:T(8,128)(2,1)}, u32[]{:S(2)}) copy-start(bf16[16,128,128]{2,1,0:T(8,128)(2,1)} %param.13) | copy-start | bytes 1572868
where the time goes:
time: 206 us; the launch traced here: 205 us
  blocking collectives  80.5 us (39%)
  local copies, waits for them, and re-layouts  78.6 us (38%)
  matrix products  28.4 us (14%)
  starting transfers between devices  13.6 us (7%)
  other arithmetic  3.23 us (2%)
    all_gather x4, blocking collectives, gather_children(): return lax.all_gather(values, 'mesh', axis=2, tiled=True)  41.7 us
    all_gather x4, blocking collectives, gather_parents(): return lax.all_gather(values, 'mesh', axis=2, tiled=True)  38.7 us
    unnamed x19, local copies, waits for them, and re-layouts  25.9 us
    gather x1, local copies, waits for them, and re-layouts, shards(): leaf_map = jnp.take(leaf_coupling, row_order[0], axis=1)  24.7 us
    dot_general x1, matrix products, shards(): jnp.einsum('mkji,cmkj->cmki', leaf_inverse, residue.astype(jnp.bfloat16)....  9.34 us
    dot_general x1, matrix products, shards(): jnp.einsum('mkij,cmkj->cmki', leaf_inverse, source.reshape(2, modes_dev,...  8.98 us
    all_to_all x1, local copies, waits for them, and re-layouts, shards(): lax.all_to_all(magnetic.astype(jnp.bfloat16), 'mode', split_axis=3, conca...  5.77 us
    all_to_all x1, local copies, waits for them, and re-layouts, shards(): lax.all_to_all(velocity.astype(jnp.bfloat16), 'mode', split_axis=3, conca...  5.77 us
  transfers between devices with their start and end apart: 3, of which 0 were waited for; matrix products, arithmetic and copies ran while one was open for 25% of the time, Pallas kernels for 0%

commit v1 on v0

--- a/solution.py
+++ b/solution.py
@@ -7,6 +7,21 @@
 NPHI = 192
 highest = lax.Precision.HIGHEST
 dt_step = 0.5
+
+
+def wait_the_yards(a0, array_dim, local_x):
+    val2 = a0.shape
+    return jnp.moveaxis(
+        a0.reshape(*val2[:array_dim], local_x, val2[array_dim] // local_x, *val2[array_dim + 1 :]),
+        array_dim,
+        0,
+    )
+
+
+def _carry_masks(point, axis_k):
+    block_out = list(point.shape[1:])
+    block_out[axis_k] *= point.shape[0]
+    return jnp.moveaxis(point, 0, axis_k).reshape(block_out)
 
 
 def tables():
@@ -59,6 +74,23 @@
     separator_source,
     front_rows,
 ):
+
+    def store_corner_by_axis(mat, device_axis, tile_in, sample=2):
+        big, wide_out = (lax.axis_size(device_axis), lax.axis_index(device_axis))
+        val = wait_the_yards(mat, tile_in, big)
+        store = [val[wide_out]]
+        for s in tuple(range(1, big)):
+            e_next = val[(wide_out + s) % big]
+            store.append(
+                lax.ppermute(
+                    e_next,
+                    axis_name=device_axis,
+                    perm=[(to_i, (to_i + s) % big) for to_i in range(big)],
+                )
+            )
+        val = jnp.stack(store)[(wide_out - jnp.arange(big)) % big]
+        return _carry_masks(val, sample)
+
     modes_dev = velocity.shape[2]
     nodes_dev = velocity.shape[3]
     forward, backward = tables()
@@ -66,9 +98,7 @@
         lax.all_to_all(
             velocity.astype(jnp.bfloat16), "mode", split_axis=3, concat_axis=2, tiled=True
         ).astype(velocity.dtype),
-        lax.all_to_all(
-            magnetic.astype(jnp.bfloat16), "mode", split_axis=3, concat_axis=2, tiled=True
-        ).astype(magnetic.dtype),
+        store_corner_by_axis(magnetic.astype(jnp.bfloat16), "mode", 3).astype(magnetic.dtype),
     )
     phys_velocity, phys_magnetic = forward_fields(forward, spread_velocity, spread_magnetic)
     local_terms = jnp.einsum(

time: 206 us -> 190 us (0.922)
  local copies, waits for them, and re-layouts: 78.6 us -> 56.9 us
  waiting for transfers between devices: 0.01 us -> 4.8 us
    unnamed x19 -> x17, local copies, waits for them, and re-layouts: 25.9 us -> 13.3 us
    ppermute x0 -> x3, starting transfers between devices: none -> 6.09 us  [store_corner_by_axis(): lax.ppermute(e_next, axis_name=device_axis, perm=[(to_i, (to_i + s) % big...]
    all_to_all x1 -> x0, local copies, waits for them, and re-layouts: 5.77 us -> none  [shards(): lax.all_to_all(magnetic.astype(jnp.bfloat16), 'mode', split_axis=3, conca...]
    all_to_all x1 -> x0, starting transfers between devices: 5.19 us -> none  [shards(): lax.all_to_all(magnetic.astype(jnp.bfloat16), 'mode', split_axis=3, conca...]
    convert_element_type x1 -> x0, local copies, waits for them, and re-layouts: 5.18 us -> none  [shards(): magnetic.astype(jnp.bfloat16)]
    all_to_all x1, waiting for transfers between devices: 0.01 us -> 4.79 us  [shards(): lax.all_to_all(velocity.astype(jnp.bfloat16), 'mode', split_axis=3, conca...]
  transfers between devices with their start and end apart: 3 -> 5, of which waited for: 0 -> 1; matrix products, arithmetic and copies ran while one was open for 25% -> 23% of each run, Pallas kernels for 0% -> 0%
where the time goes in v1:
time: 190 us; the launch traced here: 189 us
  blocking collectives  80.3 us (42%)
  local copies, waits for them, and re-layouts  56.9 us (30%)
  matrix products  28.4 us (15%)
  starting transfers between devices  13 us (7%)
  waiting for transfers between devices  4.8 us (3%)
  other arithmetic  4.55 us (2%)
    all_gather x4, blocking collectives, gather_children(): return lax.all_gather(values, 'mesh', axis=2, tiled=True)  41.7 us
    all_gather x4, blocking collectives, gather_parents(): return lax.all_gather(values, 'mesh', axis=2, tiled=True)  38.6 us
    gather x1, local copies, waits for them, and re-layouts, shards(): leaf_map = jnp.take(leaf_coupling, row_order[0], axis=1)  24.7 us
    unnamed x17, local copies, waits for them, and re-layouts  13.3 us
    dot_general x1, matrix products, shards(): jnp.einsum('mkji,cmkj->cmki', leaf_inverse, residue.astype(jnp.bfloat16)....  9.34 us
    dot_general x1, matrix products, shards(): jnp.einsum('mkij,cmkj->cmki', leaf_inverse, source.reshape(2, modes_dev,...  8.98 us
    ppermute x3, starting transfers between devices, store_corner_by_axis(): lax.ppermute(e_next, axis_name=device_axis, perm=[(to_i, (to_i + s) % big...  6.09 us
    all_to_all x1, local copies, waits for them, and re-layouts, shards(): lax.all_to_all(velocity.astype(jnp.bfloat16), 'mode', split_axis=3, conca...  5.77 us
  transfers between devices with their start and end apart: 5, of which 1 were waited for; matrix products, arithmetic and copies ran while one was open for 23% of the time, Pallas kernels for 0%

profile of v1, /device:TPU:0, one launch (start us, length us, event | category | flops | bytes accessed | tf_op | source)
XLA Modules:
  0.0 189.1 jit_solution(10231111810536779350)
XLA Ops:
  0.7 1.3 convert_element_type.163
  3.2 3.0 %collective-permute-start = (bf16[3,2,16,640]{3,2,1,0:T(8,128)(2,1)S(1)}, bf16[3,2,16,640]{3,2,1,0:T(8,128)(2,1)S(1)}, u32[]{:S(2)}, u32[]{:S(2)}) collective-permute-start(bf16[3,2,16,640]{3,2,1,0:T(8,128)(2,1)S(1)} %bitcast.217), channel_id=1, source_target_pairs={{0,8},{8,16},{16,24},{24,0},{1,9},{9,17},{17,25},{25,1},{2,10},{10... | collective-permute-start | bytes 368648 | tf_op jit(solution)/shard_map/ppermute | solution.py:85
  6.2 1.6 collective-permute-start.1
  7.8 1.5 collective-permute-start.2
  10.6 5.2 %copy.90 = bf16[3,2,16,2560]{2,0,1,3:T(4,128)(2,1)} copy(bf16[3,2,16,2560]{3,2,1,0:T(8,128)(2,1)S(1)} %convert_element_type.162) | data formatting | bytes 983040 | tf_op jit(solution)/shard_map/convert_element_type | solution.py:99
  15.8 6.7 %reshape.351 = bf16[4,2,30720]{2,1,0:T(2,128)(2,1)} reshape(bf16[2560,2,3,16]{3,2,1,0:T(4,128)(2,1)} %bitcast.205) | data formatting | bytes 983040
  22.4 3.5 %all-to-all-start = ((bf16[4,2,30720]{2,1,0:T(2,128)(2,1)}), bf16[4,2,30720]{2,1,0:T(2,128)(2,1)S(1)}, u32[]{:S(2)}, u32[]{:S(2)}) async-start(bf16[4,2,30720]{2,1,0:T(2,128)(2,1)} %reshape.351), calls=%async_computation | async-start | bytes 983040 | tf_op jit(solution)/shard_map/all_to_all | solution.py:98
  28.2 4.8 %all-to-all-done = bf16[4,2,30720]{2,1,0:T(2,128)(2,1)S(1)} async-done(((bf16[4,2,30720]{2,1,0:T(2,128)(2,1)}), bf16[4,2,30720]{2,1,0:T(2,128)(2,1)S(1)}, u32[]{:S(2)}, u32[]{:S(2)}) %all-to-all-start) | async-done | bytes 491552 | tf_op jit(solution)/shard_map/all_to_all | solution.py:98
  33.0 6.0 %reshape.352 = bf16[2560,2,3,16]{3,2,1,0:T(4,128)(2,1)} reshape(bf16[4,2,30720]{2,1,0:T(2,128)(2,1)S(1)} %all-to-all-done) | data formatting | bytes 983040
  38.9 5.8 %copy.91 = bf16[3,2,16,4,640]{4,2,3,1,0:T(8,128)(2,1)S(1)} copy(bf16[3,2,16,4,640]{2,0,1,4,3:T(4,128)(2,1)} %bitcast.206) | data formatting | bytes 983040 | tf_op jit(solution)/shard_map/all_to_all | solution.py:98
  48.2 3.5 %all-to-all-start.1 = ((bf16[3,2,64,640]{3,1,0,2:T(2,128)(2,1)}), bf16[3,2,64,640]{3,1,0,2:T(2,128)(2,1)S(1)}, u32[]{:S(2)}, u32[]{:S(2)}) async-start(bf16[3,2,64,640]{3,1,0,2:T(2,128)(2,1)} %copy.93), calls=%async_computation.1 | async-start | bytes 983040 | tf_op jit(solution)/shard_map/all_to_all | solution.py:107
  51.8 2.8 %gather_fusion.2 = bf16[128,16,128]{2,0,1:T(8,128)(2,1)S(1)} fusion(bf16[16,128,128]{2,1,0:T(8,128)(2,1)S(1)} %copy-done, s32[1024]{0:T(1024)S(1)} %pad_clamp_fusion), kind=kCustom, calls=%fused_computation.2 | custom fusion | bytes 1049088 | tf_op jit(solution)/shard_map/jit(_take)/gather | solution.py:126
  54.6 24.7 %gather_fusion.1 = bf16[128,16,2560]{2,0,1:T(8,128)(2,1)} fusion(bf16[16,128,2560]{2,1,0:T(8,128)(2,1)} %param.11, s32[1024]{0:T(1024)S(1)} %pad_clamp_fusion.1), kind=kCustom, calls=%fused_computation.1 | custom fusion | bytes 20972032 | tf_op jit(solution)/shard_map/jit(_take)/gather | solution.py:125
  81.6 9.0 %fusion.20 = bf16[2,16,2560]{2,0,1:T(2,128)(2,1)S(1)} fusion(bf16[16,20,128,128]{3,2,1,0:T(8,128)(2,1)} %param.10, bf16[2,16,20,128]{3,2,1,0:T(8,128)(2,1)S(1)} %convert_element_type.172), kind=kOutput, calls=%fused_computation.23 | convolution fusion | flops 21053440 | bytes 10813440 | tf_op jit(solution)/shard_map/mkij,cmkj->cmki/dot_general | solution.py:115
  90.6 2.9 %fusion.26 = f32[2,16,128]{2,0,1:T(2,128)S(1)} fusion(bf16[2,16,2560]{2,0,1:T(2,128)(2,1)S(1)} %fusion.20, bf16[128,16,2560]{2,0,1:T(8,128)(2,1)S(1)} %copy-done.1, pred[128]{0:T(512)(128)(4,1)S(1)} %get-tuple-element.32), kind=kOutput, calls=%fused_computation.25 | convolution fusion | flops 26214400 | bytes 10666112 | tf_op jit(solution)/shard_map/mij,cmj->cmi/dot_general | solution.py:127
  93.5 12.5 %all_gather.24 = f32[2,16,1024]{2,0,1:T(2,128)S(1)} all-gather(f32[2,16,128]{2,0,1:T(2,128)S(1)} %fusion.26), channel_id=1, replica_groups=mesh['mode'=4,'mesh'=8] {'mesh'}, dimensions={2}, use_global_device_ids=true | all-gather | bytes 147456 | tf_op jit(solution)/shard_map/all_gather | solution.py:55
  106.8 9.3 %all_gather.25 = f32[2,16,1024]{2,0,1:T(2,128)S(1)} all-gather(f32[2,16,128]{2,0,1:T(2,128)S(1)} %fusion.35), channel_id=1, replica_groups=mesh['mode'=4,'mesh'=8] {'mesh'}, dimensions={2}, use_global_device_ids=true | all-gather | bytes 147456 | tf_op jit(solution)/shard_map/all_gather | solution.py:55
  116.9 10.6 %all_gather.26 = f32[2,16,1024]{2,0,1:T(2,128)S(1)} all-gather(f32[2,16,128]{2,0,1:T(2,128)S(1)} %fusion.34), channel_id=1, replica_groups=mesh['mode'=4,'mesh'=8] {'mesh'}, dimensions={2}, use_global_device_ids=true | all-gather | bytes 147456 | tf_op jit(solution)/shard_map/all_gather | solution.py:55
  128.4 9.3 %all_gather.27 = f32[2,16,1024]{2,0,1:T(2,128)S(1)} all-gather(f32[2,16,128]{2,0,1:T(2,128)S(1)} %fusion.33), channel_id=1, replica_groups=mesh['mode'=4,'mesh'=8] {'mesh'}, dimensions={2}, use_global_device_ids=true | all-gather | bytes 147456 | tf_op jit(solution)/shard_map/all_gather | solution.py:55
  138.3 10.3 %all_gather.28 = bf16[2,16,1024]{2,0,1:T(2,128)(2,1)S(1)} all-gather(bf16[2,16,128]{2,0,1:T(2,128)(2,1)S(1)} %convert_bitcast_fusion.2), channel_id=1, replica_groups=mesh['mode'=4,'mesh'=8] {'mesh'}, dimensions={2}, use_global_device_ids=true | all-gather | bytes 73728 | tf_op jit(solution)/shard_map/all_gather | solution.py:59
  149.1 9.0 %all_gather.29 = bf16[2,16,1024]{2,0,1:T(2,128)(2,1)S(1)} all-gather(bf16[2,16,128]{2,0,1:T(2,128)(2,1)S(1)} %convert_bitcast_fusion.1), channel_id=1, replica_groups=mesh['mode'=4,'mesh'=8] {'mesh'}, dimensions={2}, use_global_device_ids=true | all-gather | bytes 73728 | tf_op jit(solution)/shard_map/all_gather | solution.py:59
  158.5 10.3 %all_gather.30 = bf16[2,16,1024]{2,0,1:T(2,128)(2,1)S(1)} all-gather(bf16[2,16,128]{2,0,1:T(2,128)(2,1)S(1)} %convert_bitcast_fusion), channel_id=1, replica_groups=mesh['mode'=4,'mesh'=8] {'mesh'}, dimensions={2}, use_global_device_ids=true | all-gather | bytes 73728 | tf_op jit(solution)/shard_map/all_gather | solution.py:59
  169.9 9.0 %all_gather.31 = bf16[2,16,1024]{2,0,1:T(2,128)(2,1)S(1)} all-gather(bf16[2,16,128]{2,0,1:T(2,128)(2,1)S(1)} %get-tuple-element.37), channel_id=1, replica_groups=mesh['mode'=4,'mesh'=8] {'mesh'}, dimensions={2}, use_global_device_ids=true | all-gather | bytes 73728 | tf_op jit(solution)/shard_map/all_gather | solution.py:59
  178.9 9.3 %convolution_bitcast_fusion.2 = f32[2,16,20,128]{3,0,2,1:T(2,128)S(1)} fusion(bf16[16,20,128,128]{3,2,1,0:T(8,128)(2,1)} %param.10, bf16[128,16,2560]{2,0,1:T(8,128)(2,1)} %gather_fusion.1, pred[128]{0:T(512)(128)(4,1)S(1)} %get-tuple-element.32, bf16[2,16,2560]{2,0,1:T(2,128)(2,1)S(1)} %fusion.20, bf16[2,16,1024]{2,0,1:T(2,128)(2,1)S(1)} %all_gather.31, ...), kind=kOutput, calls=%fused_computation.21 | convolution fusion | flops 47431680 | bytes 21471748 | tf_op jit(solution)/shard_map/mkji,cmkj->cmki/dot_general | solution.py:195
  (61 shorter events, 16.3 us)
Async XLA Ops:
  0.6 51.2 %copy-start = (bf16[16,128,128]{2,1,0:T(8,128)(2,1)S(1)}, bf16[16,128,128]{2,1,0:T(8,128)(2,1)}, u32[]{:S(2)}) copy-start(bf16[16,128,128]{2,1,0:T(8,128)(2,1)} %param.13) | copy-start | bytes 1572868
  0.6 25.5 %copy-start.4 = (s32[1,2,128]{2,1,0:T(2,128)S(1)}, s32[1,2,128]{2,1,0:T(2,128)}, u32[]{:S(2)}) copy-start(s32[1,2,128]{2,1,0:T(2,128)} %param.15) | copy-start | bytes 3076
  3.2 23.4 %collective-permute-start = (bf16[3,2,16,640]{3,2,1,0:T(8,128)(2,1)S(1)}, bf16[3,2,16,640]{3,2,1,0:T(8,128)(2,1)S(1)}, u32[]{:S(2)}, u32[]{:S(2)}) collective-permute-start(bf16[3,2,16,640]{3,2,1,0:T(8,128)(2,1)S(1)} %bitcast.217), channel_id=1, source_target_pairs={{0,8},{8,16},{16,24},{24,0},{1,9},{9,17},{17,25},{25,1},{2,10},{10... | collective-permute-start | bytes 368648 | tf_op jit(solution)/shard_map/ppermute | solution.py:85
  6.2 20.3 %collective-permute-start.1 = (bf16[3,2,16,640]{3,2,1,0:T(8,128)(2,1)S(1)}, bf16[3,2,16,640]{3,2,1,0:T(8,128)(2,1)S(1)}, u32[]{:S(2)}, u32[]{:S(2)}) collective-permute-start(bf16[3,2,16,640]{3,2,1,0:T(8,128)(2,1)S(1)} %bitcast.218), channel_id=1, source_target_pairs={{0,16},{8,24},{16,0},{24,8},{1,17},{9,25},{17,1},{25,9},{2,18},{10... | collective-permute-start | bytes 368648 | tf_op jit(solution)/shard_map/ppermute | solution.py:85
  7.8 18.7 %collective-permute-start.2 = (bf16[3,2,16,640]{3,2,1,0:T(8,128)(2,1)S(1)}, bf16[3,2,16,640]{3,2,1,0:T(8,128)(2,1)S(1)}, u32[]{:S(2)}, u32[]{:S(2)}) collective-permute-start(bf16[3,2,16,640]{3,2,1,0:T(8,128)(2,1)S(1)} %bitcast.220), channel_id=1, source_target_pairs={{0,24},{8,0},{16,8},{24,16},{1,25},{9,1},{17,9},{25,17},{2,26},{10... | collective-permute-start | bytes 368648 | tf_op jit(solution)/shard_map/ppermute | solution.py:85
  22.4 10.5 %all-to-all-start = ((bf16[4,2,30720]{2,1,0:T(2,128)(2,1)}), bf16[4,2,30720]{2,1,0:T(2,128)(2,1)S(1)}, u32[]{:S(2)}, u32[]{:S(2)}) async-start(bf16[4,2,30720]{2,1,0:T(2,128)(2,1)} %reshape.351), calls=%async_computation | async-start | bytes 983040 | tf_op jit(solution)/shard_map/all_to_all | solution.py:98
  48.2 31.1 %all-to-all-start.1 = ((bf16[3,2,64,640]{3,1,0,2:T(2,128)(2,1)}), bf16[3,2,64,640]{3,1,0,2:T(2,128)(2,1)S(1)}, u32[]{:S(2)}, u32[]{:S(2)}) async-start(bf16[3,2,64,640]{3,1,0,2:T(2,128)(2,1)} %copy.93), calls=%async_computation.1 | async-start | bytes 983040 | tf_op jit(solution)/shard_map/all_to_all | solution.py:107
  80.5 10.1 %copy-start.1 = (bf16[128,16,2560]{2,0,1:T(8,128)(2,1)S(1)}, bf16[128,16,2560]{2,0,1:T(8,128)(2,1)}, u32[]{:S(2)}) copy-start(bf16[128,16,2560]{2,0,1:T(8,128)(2,1)} %gather_fusion.1) | copy-start | bytes 31457284
  90.6 15.4 %copy-start.2 = (bf16[16,128,128]{2,1,0:T(8,128)(2,1)S(1)}, bf16[16,128,128]{2,1,0:T(8,128)(2,1)}, u32[]{:S(2)}) copy-start(bf16[16,128,128]{2,1,0:T(8,128)(2,1)} %param.12) | copy-start | bytes 1572868
  90.6 15.4 %copy-start.3 = (f32[2,16,128]{2,1,0:T(8,128)S(1)}, f32[2,16,128]{2,1,0:T(8,128)}, u32[]{:S(2)}) copy-start(f32[2,16,128]{2,1,0:T(8,128)} %param.14) | copy-start | bytes 49156
